TPU v7x, 32 devices: a 4x4x1 block of a 4x4x8 slice. The times are simulated.
32 devices in a mesh: data: 1 (over z), pp: 4 (over y), ep: 8 (over x, core).
Axes of the slice: x: 4, y: 4, z: 1, core: 2. Of those that a mesh axis runs over, the one named last changes fastest.
The devices are a block of a 4x4x8 slice.
Arguments:
- expert_out: bfloat16 [4, 1, 256, 64, 4096], P('pp', 'data', 'ep')
- expert_ids: int32 [4, 1, 8, 128, 8], P('pp', 'data', 'ep')
- slot_ids: int32 [4, 1, 8, 128, 8], P('pp', 'data', 'ep')
- gate_weights: float32 [4, 1, 8, 128, 8], P('pp', 'data', 'ep')
- residual: bfloat16 [4, 1, 8, 128, 4096], P('pp', 'data', 'ep')
- norm_moe: float32 [4, 4096], P('pp')
- w_gate: bfloat16 [4, 4096, 1024], P('pp')
- w_up: bfloat16 [4, 4096, 1024], P('pp')
- w_down: bfloat16 [4, 1024, 4096], P('pp')
- norm_attn: float32 [4, 4096], P('pp')
- w_query: bfloat16 [4, 4096, 32, 128], P('pp')
- w_key: bfloat16 [4, 4096, 32, 128], P('pp')
- w_value: bfloat16 [4, 4096, 32, 128], P('pp')
- w_out: bfloat16 [4, 32, 128, 4096], P('pp')
Outputs:
- output: bfloat16 [4, 1, 8, 128, 4096], P('pp', 'data', 'ep')
All inputs are finite; a program needn't handle non-finite values.
Results may differ from a plain program's by a relative error of at most 0.0160459.
Values are sent between devices in bfloat16 or wider.
A program may use at most 768 MiB of HBM per device.

v0:
```python
import math
import jax
import jax.numpy as jnp
from jax import lax
from jax.sharding import PartitionSpec as P

EPSILON = 1e-6


def rms_norm(tensor, gain):
    values = tensor.astype(jnp.float32)
    inv_rms = lax.rsqrt(jnp.mean(values * values, axis=-1, keepdims=True) + EPSILON)
    return values * inv_rms * gain


def shared_expert(residual, norm_moe, w_gate, w_up, w_down):
    normed = rms_norm(residual, norm_moe).astype(jnp.bfloat16)
    gate_act = jnp.einsum("bld,df->blf", normed, w_gate, preferred_element_type=jnp.float32)
    up_act = jnp.einsum("bld,df->blf", normed, w_up, preferred_element_type=jnp.float32)
    hidden = (jax.nn.silu(gate_act) * up_act).astype(jnp.bfloat16)
    return jnp.einsum("blf,fd->bld", hidden, w_down, preferred_element_type=jnp.float32).astype(jnp.bfloat16)


def gather_combine(row_table, row_ids, kept_mask, gate_weights):
    picked = jnp.take(row_table, row_ids, axis=0, mode="clip")
    weights = jnp.where(kept_mask, gate_weights, 0.0)
    return jnp.sum(picked.astype(jnp.float32) * weights[..., None], axis=-2)


def attention_block(combined, norm_attn, w_query, w_key, w_value, w_out):
    seq_len = combined.shape[1]
    score_scale = 1.0 / math.sqrt(w_query.shape[2])
    normed = rms_norm(combined, norm_attn).astype(jnp.bfloat16)
    queries = jnp.einsum("bld,dhe->blhe", normed, w_query, preferred_element_type=jnp.float32).astype(jnp.bfloat16)
    key_heads = jnp.einsum("bld,dhe->blhe", normed, w_key, preferred_element_type=jnp.float32).astype(jnp.bfloat16)
    value_heads = jnp.einsum("bld,dhe->blhe", normed, w_value, preferred_element_type=jnp.float32).astype(jnp.bfloat16)
    scores = jnp.einsum("bqhe,bkhe->bhqk", queries, key_heads, preferred_element_type=jnp.float32) * score_scale
    causal = jnp.arange(seq_len)[:, None] >= jnp.arange(seq_len)[None, :]
    scores = jnp.where(causal, scores, -1e30)
    attn_probs = jnp.exp(scores - jnp.max(scores, axis=-1, keepdims=True))
    prob_sum = jnp.sum(attn_probs, axis=-1, keepdims=True)
    attn_mixed = jnp.einsum("bhqk,bkhe->bhqe", attn_probs.astype(jnp.bfloat16), value_heads, preferred_element_type=jnp.float32) / prob_sum
    attn_proj = jnp.einsum("cirf,ife->cre", attn_mixed.astype(jnp.bfloat16), w_out, preferred_element_type=jnp.float32).astype(jnp.bfloat16)
    return (combined.astype(jnp.float32) + attn_proj.astype(jnp.float32)).astype(jnp.bfloat16)


def solution(mesh):
    stages = mesh.shape["pp"]
    ep_size = mesh.shape["ep"]
    shift_pairs = [(source, (source + 1) % stages) for source in range(stages)]
    tok_spec = P("pp", "data", "ep", None, None)
    vec_spec = P("pp", None)
    mat_spec = P("pp", None, None)
    head_spec = P("pp", None, None, None)

    def device_step(expert_out, expert_ids, slot_ids, gate_weights, residual, norm_moe, w_gate, w_up, w_down, norm_attn, w_query, w_key, w_value, w_out):
        micro_count = expert_out.shape[1]
        local_experts, slots_total, model_dim = expert_out.shape[2:]
        cap_slots = slots_total // ep_size
        first_slot = lax.axis_index("ep") * cap_slots
        results = []
        for micro_idx in range(micro_count):
            local_out = expert_out[0, micro_idx].reshape(local_experts, ep_size, cap_slots, model_dim)
            received = lax.all_to_all(local_out, "ep", 1, 0, tiled=True)
            row_table = received.reshape(local_experts * ep_size * cap_slots, model_dim)
            slot_here = slot_ids[0, micro_idx]
            kept_mask = slot_here >= 0
            row_ids = expert_ids[0, micro_idx] * cap_slots + jnp.where(kept_mask, slot_here - first_slot, 0)
            routed = gather_combine(row_table, row_ids, kept_mask, gate_weights[0, micro_idx])
            resid_here = residual[0, micro_idx]
            shared = shared_expert(resid_here, norm_moe[0], w_gate[0], w_up[0], w_down[0])
            combined = (resid_here.astype(jnp.float32) + shared.astype(jnp.float32) + routed).astype(jnp.bfloat16)
            incoming = lax.ppermute(combined, "pp", shift_pairs)
            results.append(attention_block(incoming, norm_attn[0], w_query[0], w_key[0], w_value[0], w_out[0]))
        return jnp.stack(results)[None]

    in_specs = (tok_spec,) * 5 + (vec_spec, mat_spec, mat_spec, mat_spec, vec_spec, head_spec, head_spec, head_spec, head_spec)
    return jax.shard_map(device_step, mesh=mesh, in_specs=in_specs, out_specs=tok_spec, check_vma=False)
```

profile of v0, /device:TPU:97, one launch (start us, length us, event | category | flops | bytes accessed | tf_op | source)
XLA Modules:
  0.0 360.4 jit_solution(16746851463258868004)
XLA Ops:
  0.0 14.0 %copy.17 = bf16[32,8,8,4096]{3,2,0,1:T(8,128)(2,1)} copy(bf16[32,8,8,4096]{3,2,1,0:T(8,128)(2,1)} %bitcast.110) | data formatting | bytes 33554432 | tf_op jit(solution)/shard_map/reshape;squeeze | solution.py:63
  14.0 0.0 copy-start.2
  14.0 0.0 copy-start.3
  14.0 0.0 copy-start.4
  14.0 0.0 copy-start
  14.0 0.0 copy-start.1
  14.0 7.8 %all-to-all-start = ((bf16[32,8,8,4096]{3,2,0,1:T(8,128)(2,1)}), bf16[32,8,8,4096]{3,2,0,1:T(8,128)(2,1)}, u32[]{:S(2)}, u32[]{:S(2)}) async-start(bf16[32,8,8,4096]{3,2,0,1:T(8,128)(2,1)} %copy.17), calls=%async_computation | async-start | bytes 33554432 | tf_op jit(solution)/shard_map/all_to_all | solution.py:64
  21.8 0.0 copy-done.2
  21.8 0.0 copy-done.3
  21.9 0.1 copy.18
  22.0 0.1 reshape.269
  22.0 0.0 copy-done.4
  22.1 0.1 copy.19
  22.2 0.0 copy-done
  22.2 0.3 fusion.57
  22.5 0.0 copy-done.1
  22.5 5.5 %fusion.13 = f32[128,1024]{1,0:T(8,128)} fusion(bf16[1,4096,1024]{2,1,0:T(8,128)(2,1)} %param.20, bf16[1,1,1,128,4096]{4,3,2,1,0:T(8,128)(2,1)S(1)} %copy-done, f32[4096]{0:T(1024)S(1)} %bitcast.111, f32[128]{0:T(128)S(1)} %add_rsqrt_fusion.1), kind=kOutput, calls=%fused_computation.15 | convolution fusion | flops 1075838976 | bytes 9978368 | tf_op jit(solution)/shard_map/bld,df->blf/dot_general | solution.py:18
  28.0 177.3 %all-to-all-done = bf16[32,8,8,4096]{3,2,0,1:T(8,128)(2,1)} async-done(((bf16[32,8,8,4096]{3,2,0,1:T(8,128)(2,1)}), bf16[32,8,8,4096]{3,2,0,1:T(8,128)(2,1)}, u32[]{:S(2)}, u32[]{:S(2)}) %all-to-all-start) | async-done | bytes 16777248 | tf_op jit(solution)/shard_map/all_to_all | solution.py:64
  205.3 23.4 %gather_fusion = bf16[1024,4096]{1,0:T(8,128)(2,1)} fusion(bf16[2048,4096]{1,0:T(8,128)(2,1)} %bitcast.9, s32[1024]{0:T(1024)S(1)} %broadcast_clamp_fusion), kind=kCustom, calls=%fused_computation | custom fusion | bytes 16781312 | tf_op jit(solution)/shard_map/jit(_take)/gather | solution.py:25
  228.8 11.8 %fusion.8 = f32[128,4096]{1,0:T(8,128)S(1)} fusion(bf16[1024,4096]{1,0:T(8,128)(2,1)} %gather_fusion, f32[128,8]{1,0:T(8,128)S(1)} %copy.19), kind=kLoop, calls=%fused_computation.10 | loop fusion | flops 12058624 | bytes 10489856 | tf_op jit(solution)/shard_map/reduce_sum | solution.py:27
  240.6 0.0 copy-start.5
  240.6 9.5 %fusion.36 = bf16[1,128,4096]{2,1,0:T(8,128)(2,1)} fusion(f32[128,4096]{1,0:T(8,128)S(1)} %fusion.8, bf16[1,1024,4096]{2,1,0:T(8,128)(2,1)} %param.22, bf16[1,1,1,128,4096]{4,3,2,1,0:T(8,128)(2,1)S(1)} %copy-done, bf16[1,4096,1024]{2,1,0:T(8,128)(2,1)} %param.21, f32[128,1024]{1,0:T(8,128)} %fusion.13, f32[4096]{0:T(1024)S(1)} %bitcast.112, ...), kind=kOutput, calls=%fused_computation.24 | convolution fusion | flops 2153512960 | bytes 21512704 | tf_op jit(solution)/shard_map/blf,fd->bld/dot_general | solution.py:21
  250.1 1.2 collective-permute-start
  251.3 25.0 %collective-permute-done = bf16[1,128,4096]{2,1,0:T(8,128)(2,1)S(1)} collective-permute-done((bf16[1,128,4096]{2,1,0:T(8,128)(2,1)}, bf16[1,128,4096]{2,1,0:T(8,128)(2,1)S(1)}, u32[]{:S(2)}, u32[]{:S(2)}) %collective-permute-start) | collective-permute-done | bytes 1048608 | tf_op jit(solution)/shard_map/ppermute | solution.py:73
  276.3 0.3 fusion.54
  276.6 0.0 copy-done.5
  276.6 21.7 %fusion.2 = bf16[128,32,128]{2,0,1:T(8,128)(2,1)S(1)} fusion(bf16[4096,32,128]{2,1,0:T(8,128)(2,1)} %bitcast.113, bf16[1,128,4096]{2,1,0:T(8,128)(2,1)S(1)} %collective-permute-done, f32[4096]{0:T(1024)S(1)} %bitcast.116, f32[128]{0:T(128)S(1)} %add_rsqrt_fusion), kind=kOutput, calls=%fused_computation.3 | convolution fusion | flops 4297064448 | bytes 35668480 | tf_op jit(solution)/shard_map/bld,dhe->blhe/dot_general | solution.py:36
  298.3 1.7 copy.41
  300.0 22.2 %fusion.69 = bf16[128,32,128]{2,0,1:T(8,128)(2,1)} fusion(bf16[4096,32,128]{2,1,0:T(8,128)(2,1)} %bitcast.114, bf16[1,128,4096]{2,1,0:T(8,128)(2,1)S(1)} %collective-permute-done, f32[4096]{0:T(1024)S(1)} %bitcast.117, f32[128]{0:T(128)S(1)} %add_rsqrt_fusion), kind=kOutput, calls=%fused_computation.50 | convolution fusion | flops 4297588736 | bytes 35668480 | tf_op jit(solution)/shard_map/bld,dhe->blhe/dot_general | solution.py:35
  322.2 22.4 %fusion.60 = (f32[32,128]{1,0:T(8,128)S(1)}, f32[32,128,128]{1,2,0:T(8,128)S(1)}) fusion(pred[128,128]{0,1:T(8,128)(4,1)S(1)} %iota_compare_fusion, bf16[128,32,128]{2,0,1:T(8,128)(2,1)} %fusion.69, bf16[4096,32,128]{2,1,0:T(8,128)(2,1)} %bitcast.115, bf16[1,128,4096]{2,1,0:T(8,128)(2,1)S(1)} %collective-permute-done, f32[4096]{0:T(1024)S(1)} %bitcast.118, ...), kind=kOutput, calls=%fused_computation.45 | convolution fusion | flops 4433375232 | bytes 37798400 | tf_op jit(solution)/shard_map/bqhe,bkhe->bhqk/dot_general | solution.py:37
  344.6 0.5 fusion.61
  345.1 15.0 %fusion.51 = bf16[1,1,1,128,4096]{4,3,2,1,0:T(8,128)(2,1)} fusion(bf16[1,32,128,4096]{3,2,1,0:T(8,128)(2,1)} %param.27, bf16[1,128,4096]{2,1,0:T(8,128)(2,1)S(1)} %collective-permute-done, f32[32,128,128]{1,2,0:T(8,128)S(1)} %get-tuple-element.6, bf16[128,32,128]{2,1,0:T(8,128)(2,1)} %copy.41, f32[32,128]{1,0:T(8,128)S(1)} %fusion.61, ...), kind=kOutput, calls=%fused_computation.29 | convolution fusion | flops 4434952192 | bytes 38846464 | tf_op jit(solution)/shard_map/cirf,ife->cre/dot_general | solution.py:43
  (6 shorter events, 0.0 us)
Async XLA Ops:
  14.0 7.8 %copy-start.2 = (s32[1,1,1,128,8]{3,4,2,1,0:T(8,128)S(1)}, s32[1,1,1,128,8]{3,4,2,1,0:T(8,128)}, u32[]{:S(2)}) copy-start(s32[1,1,1,128,8]{3,4,2,1,0:T(8,128)} %param.16) | copy-start | bytes 12292
  14.0 7.8 %copy-start.3 = (s32[1,1,1,128,8]{3,4,2,1,0:T(8,128)S(1)}, s32[1,1,1,128,8]{3,4,2,1,0:T(8,128)}, u32[]{:S(2)}) copy-start(s32[1,1,1,128,8]{3,4,2,1,0:T(8,128)} %param.15) | copy-start | bytes 12292
  14.0 8.1 %copy-start.4 = (f32[1,1,1,128,8]{3,4,2,1,0:T(8,128)S(1)}, f32[1,1,1,128,8]{3,4,2,1,0:T(8,128)}, u32[]{:S(2)}) copy-start(f32[1,1,1,128,8]{3,4,2,1,0:T(8,128)} %param.17) | copy-start | bytes 12292
  14.0 8.2 %copy-start = (bf16[1,1,1,128,4096]{4,3,2,1,0:T(8,128)(2,1)S(1)}, bf16[1,1,1,128,4096]{4,3,2,1,0:T(8,128)(2,1)}, u32[]{:S(2)}) copy-start(bf16[1,1,1,128,4096]{4,3,2,1,0:T(8,128)(2,1)} %param.18) | copy-start | bytes 3145732
  14.0 8.5 %copy-start.1 = (f32[1,4096]{1,0:T(1,128)S(1)}, f32[1,4096]{1,0:T(1,128)}, u32[]{:S(2)}) copy-start(f32[1,4096]{1,0:T(1,128)} %param.19) | copy-start | bytes 49156
  14.0 191.3 %all-to-all-start = ((bf16[32,8,8,4096]{3,2,0,1:T(8,128)(2,1)}), bf16[32,8,8,4096]{3,2,0,1:T(8,128)(2,1)}, u32[]{:S(2)}, u32[]{:S(2)}) async-start(bf16[32,8,8,4096]{3,2,0,1:T(8,128)(2,1)} %copy.17), calls=%async_computation | async-start | bytes 33554432 | tf_op jit(solution)/shard_map/all_to_all | solution.py:64
  240.6 36.0 %copy-start.5 = (f32[1,4096]{1,0:T(1,128)S(1)}, f32[1,4096]{1,0:T(1,128)}, u32[]{:S(2)}) copy-start(f32[1,4096]{1,0:T(1,128)} %param.23) | copy-start | bytes 49156
  250.1 26.2 %collective-permute-start = (bf16[1,128,4096]{2,1,0:T(8,128)(2,1)}, bf16[1,128,4096]{2,1,0:T(8,128)(2,1)S(1)}, u32[]{:S(2)}, u32[]{:S(2)}) collective-permute-start(bf16[1,128,4096]{2,1,0:T(8,128)(2,1)} %fusion.36), channel_id=1, source_target_pairs={{0,8},{8,16},{16,24},{24,0},{1,9},{9,17},{17,25},{25,1},{2,10},{10... | collective-permute-start | bytes 3145736 | tf_op jit(solution)/shard_map/ppermute | solution.py:73
where the time goes:
time: 366 us; the launch traced here: 360 us
  waiting for transfers between devices  202 us (55%)
  matrix products  96.3 us (26%)
  local copies, waits for them, and re-layouts  39.4 us (11%)
  other arithmetic  12.9 us (4%)
  starting transfers between devices  9.06 us (2%)
    all_to_all x1, waiting for transfers between devices, device_step(): received = lax.all_to_all(local_out, 'ep', 1, 0, tiled=True)  177 us
    ppermute x1, waiting for transfers between devices, device_step(): incoming = lax.ppermute(combined, 'pp', shift_pairs)  25 us
    gather x1, local copies, waits for them, and re-layouts, gather_combine(): picked = jnp.take(row_table, row_ids, axis=0, mode='clip')  23.4 us
    dot_general x1, matrix products, attention_block(): jnp.einsum('bqhe,bkhe->bhqk', queries, key_heads, preferred_element_type=...  22.4 us
    dot_general x1, matrix products, attention_block(): jnp.einsum('bld,dhe->blhe', normed, w_key, preferred_element_type=jnp.flo...  22.2 us
    dot_general x1, matrix products, attention_block(): jnp.einsum('bld,dhe->blhe', normed, w_value, preferred_element_type=jnp.f...  21.7 us
    dot_general x1, matrix products, attention_block(): jnp.einsum('cirf,ife->cre', attn_mixed.astype(jnp.bfloat16), w_out, prefe...  15 us
    another operation x1, local copies, waits for them, and re-layouts, device_step(): expert_out[0, micro_idx]  14 us
  transfers between devices with their start and end apart: 2, of which 2 were waited for; matrix products, arithmetic and copies ran while one was open for 2% of the time, Pallas kernels for 0%

commit v1 on v0

v1 whole, which is shorter than its diff:
```python
import functools
import math
import jax
import jax.numpy as jnp
from jax import lax
from jax.experimental import pallas as pl
from jax.experimental.pallas import tpu as pltpu
from jax.sharding import PartitionSpec as P

EPSILON = 1e-6
BF16 = jnp.bfloat16
F32 = jnp.float32
MESH = pl.DeviceIdType.MESH


def rms_norm(tensor, gain):
    values = tensor.astype(F32)
    inv_rms = lax.rsqrt(jnp.mean(values * values, axis=-1, keepdims=True) + EPSILON)
    return values * inv_rms * gain


def attention_block(combined, norm_attn, w_query, w_key, w_value, w_out):
    seq_len = combined.shape[1]
    score_scale = 1.0 / math.sqrt(w_query.shape[2])
    normed = rms_norm(combined, norm_attn).astype(BF16)
    queries = jnp.einsum("bld,dhe->blhe", normed, w_query, preferred_element_type=F32).astype(BF16)
    key_heads = jnp.einsum("bld,dhe->blhe", normed, w_key, preferred_element_type=F32).astype(BF16)
    value_heads = jnp.einsum("bld,dhe->blhe", normed, w_value, preferred_element_type=F32).astype(BF16)
    scores = jnp.einsum("bqhe,bkhe->bhqk", queries, key_heads, preferred_element_type=F32) * score_scale
    causal = jnp.arange(seq_len)[:, None] >= jnp.arange(seq_len)[None, :]
    scores = jnp.where(causal, scores, -1e30)
    attn_probs = jnp.exp(scores - jnp.max(scores, axis=-1, keepdims=True))
    prob_sum = jnp.sum(attn_probs, axis=-1, keepdims=True)
    attn_mixed = jnp.einsum("bhqk,bkhe->bhqe", attn_probs.astype(BF16), value_heads, preferred_element_type=F32) / prob_sum
    attn_proj = jnp.einsum("cirf,ife->cre", attn_mixed.astype(BF16), w_out, preferred_element_type=F32).astype(BF16)
    return (combined.astype(F32) + attn_proj.astype(F32)).astype(BF16)


def remote(src, dst, send, recv, where):
    return pltpu.make_async_remote_copy(src_ref=src, dst_ref=dst, send_sem=send, recv_sem=recv, device_id=where, device_id_type=MESH)


def combine_kernel(
    chunks, stages, chips,
    eo, ids, slots, gates, resid_hbm, gain, wg, wu, wd, yout,
    rows, part, relay, final, r_ids, r_slots, r_gates, resid, normed, gbuf, ubuf, dbuf, gacc, uacc, hidden, ysend, yin,
    s_load, s_rows, s_rowx, s_route, r_route, s_msg, r_msg, s_y, r_y, s_g, s_u, s_d,
):
    toks, dim = resid.shape
    half = dim // 2
    local_experts, cap = rows.shape[2], rows.shape[3]
    depth = 2 * local_experts * cap
    step_toks = toks // chunks
    me = lax.axis_index("ep")
    stage = lax.axis_index("pp")
    chip, core = lax.div(me, 2), lax.rem(me, 2)
    other = 1 - core

    def at_chip(offset, core_idx):
        return 2 * lax.rem(chip + offset, chips) + core_idx

    right, left, across, partner = at_chip(1, core), at_chip(chips - 1, core), at_chip(2, core), at_chip(0, other)
    nxt, prv = lax.rem(stage + 1, stages), lax.rem(stage + stages - 1, stages)

    order = (2, 1, 3, 0)
    own_loads = {}
    for k in order:
        own_loads[k] = pltpu.make_async_copy(eo.at[:, at_chip(k, core)], rows.at[k, core], s_load.at[k])
        own_loads[k].start()
    resid_load = pltpu.make_async_copy(resid_hbm, resid, s_load.at[4])
    resid_load.start()

    barrier = pltpu.get_barrier_semaphore()
    for peer in ({"ep": right}, {"ep": left}, {"ep": across}, {"ep": partner}, {"pp": nxt}, {"pp": prv}):
        pl.semaphore_signal(barrier, inc=1, device_id=peer, device_id_type=MESH)
    pl.semaphore_wait(barrier, 6)

    routing = []
    for offset in (2, 1, 3):
        slot = (chips - offset) % chips
        for n, (src, dst) in enumerate(((ids, r_ids), (slots, r_slots), (gates, r_gates))):
            copy = remote(src, dst.at[slot], s_route.at[offset, n], r_route.at[slot, n], {"ep": at_chip(offset, core)})
            copy.start()
            routing.append((slot, copy))
    row_sends = {}
    for k in order:
        row_sends[k] = remote(eo.at[:, at_chip(k, other)], rows.at[k, core], s_rows.at[k], s_rowx.at[k], {"ep": partner})
        row_sends[k].start()

    kstep = gbuf.shape[1]
    ksteps = dim // kstep
    nstep = dbuf.shape[2]
    nsteps = dim // nstep
    nbuf = gbuf.shape[0]

    def load_gu(i, slot):
        return (pltpu.make_async_copy(wg.at[pl.ds(i * kstep, kstep)], gbuf.at[slot], s_g.at[slot]),
                pltpu.make_async_copy(wu.at[pl.ds(i * kstep, kstep)], ubuf.at[slot], s_u.at[slot]))

    def load_d(i, slot):
        return pltpu.make_async_copy(wd.at[:, pl.ds(i * nstep, nstep)], dbuf.at[slot], s_d.at[slot])

    resid_load.wait()
    blk = 16

    def norm_rows(i, carry):
        at = pl.ds(pl.multiple_of(i * blk, blk), blk)
        values = resid[at, :].astype(F32)
        inv = lax.rsqrt(jnp.mean(values * values, axis=-1, keepdims=True) + EPSILON)
        normed[at, :] = (values * inv * gain[...]).astype(BF16)
        return carry

    lax.fori_loop(0, toks // blk, norm_rows, 0)

    ncol = min(512, dim)

    def partial_sum(k):
        dst = at_chip(k, core)
        if k == 0:
            e, s, g = ids[...], slots[...], gates[...]
        else:
            e, s, g = r_ids[k], r_slots[k], r_gates[k]
        where_row = jnp.where(s >= 0, (e - chip * (2 * local_experts)) * cap + s - dst * cap, -1)
        row_iota = lax.broadcasted_iota(jnp.int32, (depth, toks), 0)
        weight = jnp.zeros((depth, toks), F32)
        for j in range(e.shape[0]):
            weight = jnp.where(row_iota == where_row[j:j + 1, :], g[j:j + 1, :], weight)
        weight = weight.T
        high = weight.astype(BF16)
        rest = weight - high.astype(F32)
        mid = rest.astype(BF16)
        low = (rest - mid.astype(F32)).astype(BF16)

        def column(n, carry):
            at = pl.ds(pl.multiple_of(n * ncol, ncol), ncol)
            block = rows[k, :, :, :, at].reshape(depth, ncol)
            total = jnp.dot(high, block, preferred_element_type=F32)
            total += jnp.dot(mid, block, preferred_element_type=F32)
            total += jnp.dot(low, block, preferred_element_type=F32)
            part[k, :, at] = total
            return carry

        lax.fori_loop(0, dim // ncol, column, 0)

    lo, hi = pl.ds(0, half), pl.ds(half, half)

    def message(kind, t):
        tk = pl.ds(t * step_toks, step_toks)
        src, dst, dev = {
            0: (part.at[2, tk, lo], relay.at[0, tk], right),
            1: (part.at[2, tk, hi], relay.at[1, tk], left),
            2: (part.at[1, tk, hi], final.at[0, tk, hi], right),
            3: (part.at[3, tk, lo], final.at[1, tk, lo], left),
            4: (relay.at[0, tk], final.at[0, tk, lo], right),
            5: (relay.at[1, tk], final.at[1, tk, hi], left),
        }[kind]
        return remote(src, dst, s_msg.at[kind, t], r_msg.at[kind, t], {"ep": dev})

    def send(kind, t):
        if t < chunks:
            message(kind, t).start()

    def arrive(k):
        for slot, copy in routing:
            if slot == k:
                copy.wait_recv()
        own_loads[k].wait()
        row_sends[k].wait_recv()

    arrive(2)
    partial_sum(2)
    send(0, 0)
    send(1, 0)
    arrive(1)
    partial_sum(1)
    send(2, 0)
    send(0, 1)
    arrive(3)
    partial_sum(3)
    send(3, 0)
    send(1, 1)
    for slot in range(nbuf):
        for copy in load_gu(slot, slot):
            copy.start()
        load_d(slot, slot).start()
    own_loads[0].wait()
    row_sends[0].wait_recv()
    partial_sum(0)

    gacc[...] = jnp.zeros_like(gacc)
    uacc[...] = jnp.zeros_like(uacc)

    def gate_up(i, carry):
        slot = lax.rem(i, nbuf)
        for copy in load_gu(i, slot):
            copy.wait()
        xs = normed[:, pl.ds(pl.multiple_of(i * kstep, kstep), kstep)]
        gacc[...] += jnp.dot(xs, gbuf[slot], preferred_element_type=F32)
        uacc[...] += jnp.dot(xs, ubuf[slot], preferred_element_type=F32)

        @pl.when(i + nbuf < ksteps)
        def _():
            for copy in load_gu(i + nbuf, slot):
                copy.start()
        return carry

    lax.fori_loop(0, ksteps, gate_up, 0)
    gate_act = gacc[...]
    hidden[...] = (gate_act * jax.nn.sigmoid(gate_act) * uacc[...]).astype(BF16)

    def down(i, carry):
        slot = lax.rem(i, nbuf)
        load_d(i, slot).wait()
        at = pl.ds(pl.multiple_of(i * nstep, nstep), nstep)
        shared = jnp.dot(hidden[...], dbuf[slot], preferred_element_type=F32).astype(BF16)
        part[0, :, at] += resid[:, at].astype(F32) + shared.astype(F32)

        @pl.when(i + nbuf < nsteps)
        def _():
            load_d(i + nbuf, slot).start()
        return carry

    lax.fori_loop(0, nsteps, down, 0)

    def forward(t):
        tk = pl.ds(t * step_toks, step_toks)
        message(0, t).wait_recv()
        relay[0, tk, :] += part[1, tk, lo]
        send(4, t)
        message(1, t).wait_recv()
        relay[1, tk, :] += part[3, tk, hi]
        send(5, t)
        send(2, t + 1)
        send(3, t + 1)
        send(0, t + 2)
        send(1, t + 2)

    def shift(t):
        tk = pl.ds(t * step_toks, step_toks)
        return remote(ysend.at[tk], yin.at[tk], s_y.at[t], r_y.at[t], {"pp": nxt})

    def finish(t):
        tk = pl.ds(t * step_toks, step_toks)
        for kind in (2, 3, 4, 5):
            message(kind, t).wait_recv()
        ysend[tk, :] = (part[0, tk, :] + final[0, tk, :] + final[1, tk, :]).astype(BF16)
        shift(t).start()

    for t in range(chunks):
        forward(t)
        if t > 0:
            finish(t - 1)
    finish(chunks - 1)

    for t in range(chunks):
        shift(t).wait_recv()
    out_copy = pltpu.make_async_copy(yin, yout, s_load.at[5])
    out_copy.start()
    for slot, copy in routing:
        copy.wait_send()
    for k in order:
        row_sends[k].wait_send()
    for t in range(chunks):
        for kind in range(6):
            message(kind, t).wait_send()
        shift(t).wait_send()
    out_copy.wait()


def combine(stages, chips, eo, ids, slots, gates, resid, gain, wg, wu, wd):
    local_experts, owners, cap, dim = eo.shape
    toks = resid.shape[0]
    ff = wg.shape[1]
    chunks = 4
    nbuf = 2
    kstep, nstep = min(512, dim // nbuf), min(512, dim // nbuf)
    top_k = ids.shape[0]
    any_spec = pl.BlockSpec(memory_space=pl.ANY)
    vmem = pl.BlockSpec(memory_space=pltpu.VMEM)
    dma = pltpu.SemaphoreType.DMA
    scratch = [
        pltpu.VMEM((chips, 2, local_experts, cap, dim), BF16),
        pltpu.VMEM((chips, toks, dim), F32),
        pltpu.VMEM((2, toks, dim // 2), F32),
        pltpu.VMEM((2, toks, dim), F32),
        pltpu.VMEM((chips, top_k, toks), jnp.int32),
        pltpu.VMEM((chips, top_k, toks), jnp.int32),
        pltpu.VMEM((chips, top_k, toks), F32),
        pltpu.VMEM((toks, dim), BF16),
        pltpu.VMEM((toks, dim), BF16),
        pltpu.VMEM((nbuf, kstep, ff), BF16),
        pltpu.VMEM((nbuf, kstep, ff), BF16),
        pltpu.VMEM((nbuf, ff, nstep), BF16),
        pltpu.VMEM((toks, ff), F32),
        pltpu.VMEM((toks, ff), F32),
        pltpu.VMEM((toks, ff), BF16),
        pltpu.VMEM((toks, dim), BF16),
        pltpu.VMEM((toks, dim), BF16),
        dma((6,)), dma((chips,)), dma((chips,)), dma((chips, 3)), dma((chips, 3)),
        dma((6, chunks)), dma((6, chunks)), dma((chunks,)), dma((chunks,)),
        dma((nbuf,)), dma((nbuf,)), dma((nbuf,)),
    ]
    return pl.pallas_call(
        functools.partial(combine_kernel, chunks, stages, chips),
        out_shape=jax.ShapeDtypeStruct((toks, dim), BF16),
        in_specs=[any_spec, vmem, vmem, vmem, any_spec, vmem, any_spec, any_spec, any_spec],
        out_specs=any_spec,
        scratch_shapes=scratch,
        cost_estimate=pl.CostEstimate(flops=20_000_000_000, bytes_accessed=50_000_000, transcendentals=0),
        compiler_params=pltpu.CompilerParams(collective_id=0, has_side_effects=True, vmem_limit_bytes=60 * 2**20),
        name="combine",
    )(eo, ids, slots, gates, resid, gain, wg, wu, wd)


def solution(mesh):
    stages = mesh.shape["pp"]
    ep_size = mesh.shape["ep"]
    tok_spec = P("pp", "data", "ep", None, None)
    vec_spec = P("pp", None)
    mat_spec = P("pp", None, None)
    head_spec = P("pp", None, None, None)

    def device_step(expert_out, expert_ids, slot_ids, gate_weights, residual, norm_moe, w_gate, w_up, w_down, norm_attn, w_query, w_key, w_value, w_out):
        local_experts, slots_total, model_dim = expert_out.shape[2:]
        cap = slots_total // ep_size
        eo = expert_out[0, 0].reshape(local_experts, ep_size, cap, model_dim)
        toks = residual.shape[3]

        def flip(array):
            return jnp.swapaxes(array[0, 0].reshape(toks, -1), 0, 1)

        incoming = combine(stages, ep_size // 2, eo, flip(expert_ids), flip(slot_ids), flip(gate_weights),
                           residual[0, 0, 0], norm_moe, w_gate[0], w_up[0], w_down[0])
        out = attention_block(incoming[None], norm_attn[0], w_query[0], w_key[0], w_value[0], w_out[0])
        return out[None, None]

    in_specs = (tok_spec,) * 5 + (vec_spec, mat_spec, mat_spec, mat_spec, vec_spec, head_spec, head_spec, head_spec, head_spec)
    return jax.shard_map(device_step, mesh=mesh, in_specs=in_specs, out_specs=tok_spec, check_vma=False)
```

time: 366 us -> 186 us (0.51); the launches traced: 360 us -> 186 us
  waiting for transfers between devices: 202 us -> 0 us
  Pallas kernels: 0 us -> 98.6 us
  local copies, waits for them, and re-layouts: 39.4 us -> 2.9 us
  matrix products: 96.3 us -> 82.5 us
  other arithmetic: 12.9 us -> 2.03 us
  starting transfers between devices: 9.06 us -> 0 us
    all_to_all x1 -> x0, waiting for transfers between devices: 177 us -> none  [device_step(): received = lax.all_to_all(local_out, 'ep', 1, 0, tiled=True)]
    pallas_call x0 -> x1, Pallas kernels: none -> 98.6 us  [combine(): pl.pallas_call(functools.partial(combine_kernel, chunks, stages, chips),...]
    ppermute x1 -> x0, waiting for transfers between devices: 25 us -> none  [device_step(): incoming = lax.ppermute(combined, 'pp', shift_pairs)]
    gather x1 -> x0, local copies, waits for them, and re-layouts: 23.4 us -> none  [gather_combine(): picked = jnp.take(row_table, row_ids, axis=0, mode='clip')]
    another operation x1 -> x0, local copies, waits for them, and re-layouts: 14 us -> none  [device_step(): expert_out[0, micro_idx]]
    dot_general x5 -> x3, matrix products: 73.9 us -> 60.1 us  [the longest x1 22.6 us: attention_block(): jnp.einsum('bld,dhe->blhe', normed, w_key, preferred_element_type=F32)]
    reduce_sum x1 -> x0, other arithmetic: 11.8 us -> none  [gather_combine(): return jnp.sum(picked.astype(jnp.float32) * weights[..., None], axis=-2)]
    all_to_all x1 -> x0, starting transfers between devices: 7.82 us -> none  [device_step(): received = lax.all_to_all(local_out, 'ep', 1, 0, tiled=True)]
  transfers between devices with their start and end apart: 2 -> 0, of which waited for: 2 -> 0; matrix products, arithmetic and copies ran while one was open for 2% -> 0% of each run, Pallas kernels for 0% -> 0%
where the time goes in v1:
time: 186 us
  Pallas kernels  98.6 us (53%)
  matrix products  82.5 us (44%)
  local copies, waits for them, and re-layouts  2.9 us (2%)
  other arithmetic  2.03 us (1%)
    pallas_call x1, Pallas kernels, combine(): pl.pallas_call(functools.partial(combine_kernel, chunks, stages, chips),...  98.6 us
    dot_general x1, matrix products, attention_block(): jnp.einsum('bld,dhe->blhe', normed, w_key, preferred_element_type=F32)  22.6 us
    dot_general x1, matrix products, attention_block(): jnp.einsum('bld,dhe->blhe', normed, w_value, preferred_element_type=F32)  22.5 us
    dot_general x1, matrix products, attention_block(): jnp.einsum('bqhe,bkhe->bhqk', queries, key_heads, preferred_element_type=...  22.4 us
    dot_general x1, matrix products, attention_block(): jnp.einsum('cirf,ife->cre', attn_mixed.astype(BF16), w_out, preferred_ele...  15 us

profile of v1, /device:TPU:97, one launch (start us, length us, event | category | flops | bytes accessed | tf_op | source)
XLA Modules:
  0.0 186.1 jit_solution(16109481103171090925)
XLA Ops:
  0.0 0.0 copy-start.1
  0.0 98.6 %combine.1 = bf16[128,4096]{1,0:T(8,128)(2,1)} custom-call(bf16[32,8,8,4096]{3,2,1,0:T(8,128)(2,1)} %bitcast.59, s32[8,128]{1,0:T(8,128)} %bitcast.67, s32[8,128]{1,0:T(8,128)} %bitcast.68, f32[8,128]{1,0:T(8,128)} %bitcast.69, bf16[128,4096]{1,0:T(8,128)(2,1)} %bitcast.63, f32[1,4096]{1,0:T(1,128)} %gain.1, bf16[4096,1024]{1,0:T(8,128)(2,1)} %bitcast.60, ...), custom_call_target="tpu_custom_call" | custom-call | flops 20000000000 | bytes 50000000 | tf_op jit(solution)/shard_map/combine/pallas_call | solution.py:303
  98.7 1.5 fusion.26
  100.2 0.0 copy-done.1
  100.2 0.0 copy-start
  100.2 22.6 %fusion.38 = bf16[128,32,128]{2,0,1:T(8,128)(2,1)} fusion(bf16[4096,32,128]{2,1,0:T(8,128)(2,1)} %bitcast.56, bf16[128,4096]{1,0:T(8,128)(2,1)} %combine.1, f32[4096]{0:T(1024)S(1)} %bitcast.64, f32[128]{0:T(128)S(1)} %add_rsqrt_fusion), kind=kOutput, calls=%fused_computation.28 | convolution fusion | flops 4297588736 | bytes 35668480 | tf_op jit(solution)/shard_map/bld,dhe->blhe/dot_general | solution.py:27
  122.8 0.0 copy-done
  122.8 22.4 %fusion.29 = (f32[32,128]{1,0:T(8,128)S(1)}, f32[32,128,128]{1,2,0:T(8,128)S(1)}) fusion(pred[128,128]{0,1:T(8,128)(4,1)S(1)} %iota_compare_fusion, bf16[128,32,128]{2,0,1:T(8,128)(2,1)} %fusion.38, bf16[4096,32,128]{2,1,0:T(8,128)(2,1)} %bitcast.57, bf16[128,4096]{1,0:T(8,128)(2,1)S(1)} %copy-done, f32[4096]{0:T(1024)S(1)} %bitcast.65, ...), kind=kOutput, calls=%fused_computation.23 | convolution fusion | flops 4433375232 | bytes 37798400 | tf_op jit(solution)/shard_map/bqhe,bkhe->bhqk/dot_general | solution.py:29
  145.2 22.5 %fusion.2 = bf16[128,32,128]{2,0,1:T(8,128)(2,1)} fusion(bf16[4096,32,128]{2,1,0:T(8,128)(2,1)} %bitcast.58, bf16[128,4096]{1,0:T(8,128)(2,1)S(1)} %copy-done, f32[4096]{0:T(1024)S(1)} %bitcast.66, f32[128]{0:T(128)S(1)} %add_rsqrt_fusion), kind=kOutput, calls=%fused_computation.2 | convolution fusion | flops 4297064448 | bytes 35668480 | tf_op jit(solution)/shard_map/bld,dhe->blhe/dot_general | solution.py:28
  167.7 2.9 %copy.36 = bf16[128,32,128]{2,1,0:T(8,128)(2,1)} copy(bf16[128,32,128]{2,0,1:T(8,128)(2,1)} %fusion.2) | data formatting | bytes 2097152 | tf_op jit(solution)/shard_map/bld,dhe->blhe/dot_general | solution.py:28
  170.6 0.5 fusion.30
  171.0 15.0 %fusion.23 = bf16[1,1,1,128,4096]{4,3,2,1,0:T(8,128)(2,1)} fusion(bf16[1,32,128,4096]{3,2,1,0:T(8,128)(2,1)} %param.27, bf16[128,4096]{1,0:T(8,128)(2,1)S(1)} %copy-done, f32[32,128,128]{1,2,0:T(8,128)S(1)} %get-tuple-element.6, bf16[128,32,128]{2,1,0:T(8,128)(2,1)} %copy.36, f32[32,128]{1,0:T(8,128)S(1)} %fusion.30, f32[32,128]{1,0:T(8,128)S(1)} %get-tuple-element.5, ...), kind=kOutput, calls=%fused_computation.13 | convolution fusion | flops 4434952192 | bytes 38846464 | tf_op jit(solution)/shard_map/cirf,ife->cre/dot_general | solution.py:35
  (2 shorter events, 0.0 us)
Async XLA Ops:
  0.0 100.2 %copy-start.1 = (f32[1,4096]{1,0:T(1,128)S(1)}, f32[1,4096]{1,0:T(1,128)}, u32[]{:S(2)}) copy-start(f32[1,4096]{1,0:T(1,128)} %param.23) | copy-start | bytes 49156
  100.2 22.6 %copy-start = (bf16[128,4096]{1,0:T(8,128)(2,1)S(1)}, bf16[128,4096]{1,0:T(8,128)(2,1)}, u32[]{:S(2)}) copy-start(bf16[128,4096]{1,0:T(8,128)(2,1)} %combine.1) | copy-start | bytes 3145732

commit v2 on v1

v2 whole, which is shorter than its diff:
```python
import functools
import math
import jax
import jax.numpy as jnp
from jax import lax
from jax.experimental import pallas as pl
from jax.experimental.pallas import tpu as pltpu
from jax.sharding import PartitionSpec as P

EPSILON = 1e-6
BF16 = jnp.bfloat16
F32 = jnp.float32
MESH = pl.DeviceIdType.MESH


def remote(src, dst, send, recv, where):
    return pltpu.make_async_remote_copy(src_ref=src, dst_ref=dst, send_sem=send, recv_sem=recv, device_id=where, device_id_type=MESH)


def stage_kernel(
    chunks, stages, chips,
    eo, ids, slots, gates, resid_hbm, gain_moe, gain_attn, wg, wu, wd, wq, wk, wv, wo, out_hbm,
    pool, nat, part, relay, final, r_ids, r_slots, r_gates, resid, normed, hidden, ysend, yin, kbuf,
    s_load, s_pool, s_nat, s_rows, s_rowx, s_route, r_route, s_msg, r_msg, s_y, r_y,
):
    toks, dim = resid.shape
    half = dim // 2
    groups = pool.shape[1]
    local_experts = groups // 2
    cap = pool.shape[2]
    depth = groups * cap
    step_toks = toks // chunks
    head_dim = nat.shape[3]
    half_heads = nat.shape[2]
    ksteps = dim // depth
    slabs = 2 * ksteps
    ff = wg.shape[2]
    fsteps = ff // depth
    nat_slots = nat.shape[0]
    me = lax.axis_index("ep")
    stage = lax.axis_index("pp")
    chip, core = lax.div(me, 2), lax.rem(me, 2)
    other = 1 - core

    def at_chip(offset, core_idx):
        return 2 * lax.rem(chip + offset, chips) + core_idx

    right, left, across, partner = at_chip(1, core), at_chip(chips - 1, core), at_chip(2, core), at_chip(0, other)
    nxt, prv = lax.rem(stage + 1, stages), lax.rem(stage + stages - 1, stages)
    order = (2, 1, 3, 0)
    halves = (pl.ds(0, half), pl.ds(half, half))
    lo, hi = halves

    own_loads = {}
    for k in order:
        own_loads[k] = [pltpu.make_async_copy(eo.at[:, at_chip(k, core), :, halves[h]],
                                              pool.at[2 * k + h, pl.ds(core * local_experts, local_experts)], s_load.at[2 * k + h])
                        for h in range(2)]
    for copy in own_loads[2]:
        copy.start()
    resid_load = pltpu.make_async_copy(resid_hbm, resid, s_load.at[2 * chips])
    resid_load.start()

    barrier = pltpu.get_barrier_semaphore()
    for peer in ({"ep": right}, {"ep": left}, {"ep": across}, {"ep": partner}, {"pp": nxt}, {"pp": prv}):
        pl.semaphore_signal(barrier, inc=1, device_id=peer, device_id_type=MESH)
    pl.semaphore_wait(barrier, 6)

    routing = []
    for offset in (2, 1, 3):
        slot = (chips - offset) % chips
        for n, (src, dst) in enumerate(((ids, r_ids), (slots, r_slots), (gates, r_gates))):
            copy = remote(src, dst.at[slot], s_route.at[offset, n], r_route.at[slot, n], {"ep": at_chip(offset, core)})
            copy.start()
            routing.append((slot, copy))
    row_sends = {}
    for k in order:
        row_sends[k] = [remote(eo.at[:, at_chip(k, other), :, halves[h]],
                               pool.at[2 * k + h, pl.ds(core * local_experts, local_experts)],
                               s_rows.at[2 * k + h], s_rowx.at[2 * k + h], {"ep": partner})
                        for h in range(2)]
    for copy in row_sends[2]:
        copy.start()
    for k in order[1:]:
        for copy in own_loads[k]:
            copy.start()

    first_shared = 2 * chips

    def load_gate_up(i):
        slot = first_shared + i
        at = pl.ds(i * groups, groups)
        return (pltpu.make_async_copy(wg.at[at], pool.at[slot, :, :, pl.ds(0, ff)], s_pool.at[0, slot]),
                pltpu.make_async_copy(wu.at[at], pool.at[slot, :, :, pl.ds(ff, ff)], s_pool.at[1, slot]))

    def load_rows(matrix, hh, i, slot):
        return pltpu.make_async_copy(matrix.at[pl.ds(i * groups, groups), :, pl.ds(pl.multiple_of(hh * half, half), half)],
                                     pool.at[slot], s_pool.at[0, slot])

    def load_heads(matrix, j, slot):
        hh, i = lax.div(j, ksteps), lax.rem(j, ksteps)
        return pltpu.make_async_copy(matrix.at[pl.ds(i * depth, depth), pl.ds(pl.multiple_of(hh * half_heads, half_heads), half_heads)],
                                     nat.at[slot], s_nat.at[slot])

    blk = min(16, step_toks)

    def norm_rows(src, gain, i):
        at = pl.ds(pl.multiple_of(i * blk, blk), blk)
        values = src[at, :].astype(F32)
        inv = lax.rsqrt(jnp.mean(values * values, axis=-1, keepdims=True) + EPSILON)
        normed[at, :] = (values * inv * gain[...]).astype(BF16)

    resid_load.wait()

    def norm_resid(i, carry):
        norm_rows(resid, gain_moe, i)
        return carry

    lax.fori_loop(0, toks // blk, norm_resid, 0)

    ncol = min(512, half)

    def partial_sum(k):
        dst = at_chip(k, core)
        if k == 0:
            e, s, g = ids[...], slots[...], gates[...]
        else:
            e, s, g = r_ids[k], r_slots[k], r_gates[k]
        where_row = jnp.where(s >= 0, (e - chip * (2 * local_experts)) * cap + s - dst * cap, -1)
        row_iota = lax.broadcasted_iota(jnp.int32, (depth, toks), 0)
        weight = jnp.zeros((depth, toks), F32)
        for j in range(e.shape[0]):
            weight = jnp.where(row_iota == where_row[j:j + 1, :], g[j:j + 1, :], weight)
        weight = weight.T
        high = weight.astype(BF16)
        rest = weight - high.astype(F32)
        mid = rest.astype(BF16)
        low = (rest - mid.astype(F32)).astype(BF16)
        for h in range(2):
            def column(n, carry):
                start = pl.multiple_of(n * ncol, ncol)
                block = pool[2 * k + h, :, :, pl.ds(start, ncol)].reshape(depth, ncol)
                total = jnp.dot(high, block, preferred_element_type=F32)
                total += jnp.dot(mid, block, preferred_element_type=F32)
                total += jnp.dot(low, block, preferred_element_type=F32)
                part[k, :, pl.ds(pl.multiple_of(h * half + start, ncol), ncol)] = total
                return carry

            lax.fori_loop(0, half // ncol, column, 0)

    def message(kind, t):
        tk = pl.ds(t * step_toks, step_toks)
        src, dst, dev = {
            0: (part.at[2, tk, lo], relay.at[0, tk], right),
            1: (part.at[2, tk, hi], relay.at[1, tk], left),
            2: (part.at[1, tk, hi], final.at[0, tk, hi], right),
            3: (part.at[3, tk, lo], final.at[1, tk, lo], left),
            4: (relay.at[0, tk], final.at[0, tk, lo], right),
            5: (relay.at[1, tk], final.at[1, tk, hi], left),
        }[kind]
        return remote(src, dst, s_msg.at[kind, t], r_msg.at[kind, t], {"ep": dev})

    def send(kind, t):
        if t < chunks:
            message(kind, t).start()

    def arrive(k, following):
        for slot, copy in routing:
            if slot == k:
                copy.wait_recv()
        for copy in own_loads[k]:
            copy.wait()
        for copy in row_sends[k]:
            copy.wait_recv()
        if following is not None:
            for copy in row_sends[following]:
                copy.start()

    ahead = min(3, chunks)
    arrive(2, 1)
    for i in range(ksteps):
        for copy in load_gate_up(i):
            copy.start()
    partial_sum(2)
    for t in range(ahead):
        send(0, t)
        send(1, t)
    arrive(1, 3)
    partial_sum(1)
    send(2, 0)
    arrive(3, 0)
    partial_sum(3)
    send(3, 0)
    for n in range(2 * fsteps):
        load_rows(wd, n // fsteps, n % fsteps, 4 + n).start()

    for i in range(ksteps):
        for copy in load_gate_up(i):
            copy.wait()
        product = jnp.dot(normed[:, i * depth:(i + 1) * depth], pool[first_shared + i].reshape(depth, half), preferred_element_type=F32)
        part[0, :, lo] = product if i == 0 else part[0, :, lo] + product
    gate_act = part[0, :, pl.ds(0, ff)]
    hidden[...] = (gate_act * jax.nn.sigmoid(gate_act) * part[0, :, pl.ds(ff, ff)]).astype(BF16)
    arrive(0, None)
    partial_sum(0)
    for hh in range(2):
        for i in range(fsteps):
            load_rows(wd, hh, i, 4 + hh * fsteps + i).wait()
        for n in range(half // ncol):
            at = pl.ds(hh * half + n * ncol, ncol)
            product = None
            for i in range(fsteps):
                block = pool[4 + hh * fsteps + i, :, :, pl.ds(n * ncol, ncol)].reshape(depth, ncol)
                term = jnp.dot(hidden[:, i * depth:(i + 1) * depth], block, preferred_element_type=F32)
                product = term if product is None else product + term
            part[0, :, at] += resid[:, at].astype(F32) + product.astype(BF16).astype(F32)

    def forward(t):
        tk = pl.ds(t * step_toks, step_toks)
        message(0, t).wait_recv()
        relay[0, tk, :] += part[1, tk, lo]
        send(4, t)
        message(1, t).wait_recv()
        relay[1, tk, :] += part[3, tk, hi]
        send(5, t)
        send(2, t + 1)
        send(3, t + 1)
        send(0, t + ahead)
        send(1, t + ahead)

    def shift(t):
        tk = pl.ds(t * step_toks, step_toks)
        return remote(ysend.at[tk], yin.at[tk], s_y.at[t], r_y.at[t], {"pp": nxt})

    def finish(t):
        tk = pl.ds(t * step_toks, step_toks)
        for kind in (2, 3, 4, 5):
            message(kind, t).wait_recv()
        ysend[tk, :] = (part[0, tk, :] + final[0, tk, :] + final[1, tk, :]).astype(BF16)
        shift(t).start()

    def receive(t):
        shift(t).wait_recv()
        for i in range(step_toks // blk):
            norm_rows(yin, gain_attn, t * (step_toks // blk) + i)

    for slot in range(nat_slots):
        load_heads(wq, slot, slot).start()

    def lay_out(j, carry):
        slot = lax.rem(j, nat_slots)
        load_heads(wq, j, slot).wait()
        pool[j] = nat[slot].reshape(groups, cap, half)

        @pl.when(j + nat_slots < slabs)
        def _():
            load_heads(wq, j + nat_slots, slot).start()

        @pl.when(j + nat_slots >= slabs)
        def _():
            load_heads(wk, j + nat_slots - slabs, slot).start()
        return carry

    per_chunk = -(-slabs // max(1, chunks - 2))
    done = 0
    for t in range(chunks):
        forward(t)
        if t > 0:
            finish(t - 1)
        if t > 1:
            receive(t - 2)
        upto = min(slabs, done + per_chunk) if t < chunks - 1 else slabs
        if upto > done:
            lax.fori_loop(done, upto, lay_out, 0)
        done = upto
    if chunks > 1:
        receive(chunks - 2)
    finish(chunks - 1)
    for t in range(chunks):
        for kind in range(6):
            message(kind, t).wait_send()
    part[1] = jnp.zeros((toks, dim), F32)
    part[2] = jnp.zeros((toks, dim), F32)
    part[3] = jnp.zeros((toks, dim), F32)
    receive(chunks - 1)

    qbuf, vbuf = resid, ysend

    def query(i, carry):
        for hh in range(2):
            at = halves[hh]
            product = jnp.dot(normed[:, pl.ds(pl.multiple_of(i * depth, depth), depth)], pool[hh * ksteps + i].reshape(depth, half), preferred_element_type=F32)
            part[1, :, at] += product
        load_rows(wo, 0, i, i).start()
        return carry

    lax.fori_loop(0, ksteps, query, 0)
    qbuf[...] = part[1].astype(BF16)

    def slot_of(index):
        return lax.rem(index, nat_slots)

    def stream(which, matrix, following):
        for hh in range(2):
            at = halves[hh]

            def step(i, carry):
                j = hh * ksteps + i
                slot = slot_of(j + (1 + which) * slabs)
                load_heads(matrix, j, slot).wait()
                part[2 + which, :, at] += jnp.dot(normed[:, pl.ds(pl.multiple_of(i * depth, depth), depth)], nat[slot].reshape(depth, half), preferred_element_type=F32)
                nj = j + nat_slots

                @pl.when(nj < slabs)
                def _():
                    load_heads(matrix, nj, slot).start()

                if following is not None:
                    @pl.when(nj >= slabs)
                    def _():
                        load_heads(following, nj - slabs, slot).start()

                if which == 0 and hh == 0:
                    load_rows(wo, 1, i, ksteps + i).start()
                return carry

            lax.fori_loop(0, ksteps, step, 0)

    stream(0, wk, wv)
    kbuf[...] = part[2].astype(BF16)
    stream(1, wv, None)
    for t in range(chunks):
        shift(t).wait_send()
    vbuf[...] = part[3].astype(BF16)

    scale = 1.0 / math.sqrt(head_dim)
    causal = lax.broadcasted_iota(jnp.int32, (toks, toks), 0) >= lax.broadcasted_iota(jnp.int32, (toks, toks), 1)
    together = 4

    def heads(n, carry):
        cols = [pl.ds(pl.multiple_of((n * together + m) * head_dim, head_dim), head_dim) for m in range(together)]
        scores = [lax.dot_general(qbuf[:, at], kbuf[:, at], (((1,), (1,)), ((), ())), preferred_element_type=F32) for at in cols]
        scores = [jnp.where(causal, s * scale, -1e30) for s in scores]
        probs = [jnp.exp(s - jnp.max(s, axis=-1, keepdims=True)) for s in scores]
        sums = [jnp.sum(p, axis=-1, keepdims=True) for p in probs]
        mixed = [jnp.dot(p.astype(BF16), vbuf[:, at], preferred_element_type=F32) for p, at in zip(probs, cols)]
        for at, value, total in zip(cols, mixed, sums):
            qbuf[:, at] = (value / total).astype(BF16)
        return carry

    lax.fori_loop(0, dim // (head_dim * together), heads, 0)

    out_copies = []
    for hh in range(2):
        at = halves[hh]
        for i in range(ksteps):
            load_rows(wo, hh, i, hh * ksteps + i).wait()
        for n in range(half // ncol):
            cols = pl.ds(hh * half + n * ncol, ncol)

            def proj(i, total):
                block = pool[hh * ksteps + i, :, :, pl.ds(n * ncol, ncol)].reshape(depth, ncol)
                return total + jnp.dot(qbuf[:, pl.ds(pl.multiple_of(i * depth, depth), depth)], block, preferred_element_type=F32)

            total = jnp.zeros((toks, ncol), F32)
            for i in range(ksteps):
                total = proj(i, total)
            kbuf[:, cols] = (yin[:, cols].astype(F32) + total.astype(BF16).astype(F32)).astype(BF16)
        copy = pltpu.make_async_copy(kbuf.at[:, at], out_hbm.at[:, at], s_load.at[hh])
        copy.start()
        out_copies.append(copy)

    for slot, copy in routing:
        copy.wait_send()
    for k in order:
        for copy in row_sends[k]:
            copy.wait_send()
    for copy in out_copies:
        copy.wait()


def run_stage(stages, chips, eo, ids, slots, gates, resid, gain_moe, gain_attn, wg, wu, wd, wq, wk, wv, wo):
    local_experts, owners, cap, dim = eo.shape
    toks = resid.shape[0]
    heads, head_dim = wq.shape[1:]
    ff = wg.shape[1]
    groups = 2 * local_experts
    depth = groups * cap
    half = dim // 2
    chunks = 8
    nat_slots = 4
    top_k = ids.shape[0]
    pool_slots = max(2 * dim // depth, 2 * chips + dim // depth)
    any_spec = pl.BlockSpec(memory_space=pl.ANY)
    vmem = pl.BlockSpec(memory_space=pltpu.VMEM)
    dma = pltpu.SemaphoreType.DMA
    scratch = [
        pltpu.VMEM((pool_slots, groups, cap, half), BF16),
        pltpu.VMEM((nat_slots, depth, heads // 2, head_dim), BF16),
        pltpu.VMEM((chips, toks, dim), F32),
        pltpu.VMEM((2, toks, half), F32),
        pltpu.VMEM((2, toks, dim), F32),
        pltpu.VMEM((chips, top_k, toks), jnp.int32),
        pltpu.VMEM((chips, top_k, toks), jnp.int32),
        pltpu.VMEM((chips, top_k, toks), F32),
        pltpu.VMEM((toks, dim), BF16),
        pltpu.VMEM((toks, dim), BF16),
        pltpu.VMEM((toks, ff), BF16),
        pltpu.VMEM((toks, dim), BF16),
        pltpu.VMEM((toks, dim), BF16),
        pltpu.VMEM((toks, dim), BF16),
        dma((2 * chips + 1,)), dma((2, pool_slots)), dma((nat_slots,)), dma((2 * chips,)), dma((2 * chips,)),
        dma((chips, 3)), dma((chips, 3)), dma((6, chunks)), dma((6, chunks)), dma((chunks,)), dma((chunks,)),
    ]

    def grouped(matrix):
        return matrix.reshape(-1, cap, matrix.shape[-1])

    return pl.pallas_call(
        functools.partial(stage_kernel, chunks, stages, chips),
        out_shape=jax.ShapeDtypeStruct((toks, dim), BF16),
        in_specs=[any_spec, vmem, vmem, vmem, any_spec, vmem, vmem] + [any_spec] * 7,
        out_specs=any_spec,
        scratch_shapes=scratch,
        cost_estimate=pl.CostEstimate(flops=40_000_000_000, bytes_accessed=180_000_000, transcendentals=0),
        compiler_params=pltpu.CompilerParams(collective_id=0, has_side_effects=True, vmem_limit_bytes=67_043_328),
        name="stage",
    )(eo, ids, slots, gates, resid, gain_moe, gain_attn, grouped(wg), grouped(wu), grouped(wd), wq, wk, wv, grouped(wo))


def solution(mesh):
    stages = mesh.shape["pp"]
    ep_size = mesh.shape["ep"]
    tok_spec = P("pp", "data", "ep", None, None)
    vec_spec = P("pp", None)
    mat_spec = P("pp", None, None)
    head_spec = P("pp", None, None, None)

    def device_step(expert_out, expert_ids, slot_ids, gate_weights, residual, norm_moe, w_gate, w_up, w_down, norm_attn, w_query, w_key, w_value, w_out):
        local_experts, slots_total, model_dim = expert_out.shape[2:]
        cap = slots_total // ep_size
        eo = expert_out[0, 0].reshape(local_experts, ep_size, cap, model_dim)
        toks = residual.shape[3]

        def flip(array):
            return jnp.swapaxes(array[0, 0].reshape(toks, -1), 0, 1)

        out = run_stage(stages, ep_size // 2, eo, flip(expert_ids), flip(slot_ids), flip(gate_weights), residual[0, 0, 0],
                        norm_moe, norm_attn, w_gate[0], w_up[0], w_down[0], w_query[0], w_key[0], w_value[0],
                        w_out[0].reshape(-1, model_dim))
        return out[None, None, None]

    in_specs = (tok_spec,) * 5 + (vec_spec, mat_spec, mat_spec, mat_spec, vec_spec, head_spec, head_spec, head_spec, head_spec)
    return jax.shard_map(device_step, mesh=mesh, in_specs=in_specs, out_specs=tok_spec, check_vma=False)
```

time: 186 us -> 145 us (0.78)
  matrix products: 82.5 us -> 0 us
  Pallas kernels: 98.6 us -> 143 us
  other arithmetic: 2.03 us -> 0 us
    dot_general x4 -> x0, matrix products: 82.5 us -> none  [the longest x1 22.6 us: attention_block(): jnp.einsum('bld,dhe->blhe', normed, w_key, preferred_element_type=F32)]
    pallas_call x1, Pallas kernels: 98.6 us -> 143 us  [run_stage(): pl.pallas_call(functools.partial(stage_kernel, chunks, stages, chips), ou...]
    dot_general x1 -> x0, local copies, waits for them, and re-layouts: 2.89 us -> none  [attention_block(): jnp.einsum('bld,dhe->blhe', normed, w_value, preferred_element_type=F32)]
    unnamed x4 -> x1, local copies, waits for them, and re-layouts: 0.01 us -> 2.29 us
    reduce_sum x2 -> x0, other arithmetic: 2 us -> none  [the longest x1 1.52 us: rms_norm(): jnp.mean(values * values, axis=-1, keepdims=True) + EPSILON]
where the time goes in v2:
time: 145 us
  Pallas kernels  143 us (99%)
  local copies, waits for them, and re-layouts  2.29 us (2%)
    pallas_call x1, Pallas kernels, run_stage(): pl.pallas_call(functools.partial(stage_kernel, chunks, stages, chips), ou...  143 us

profile of v2, /device:TPU:97, one launch (start us, length us, event | category | flops | bytes accessed | tf_op | source)
XLA Modules:
  0.0 145.2 jit_solution(9007410797713195393)
XLA Ops:
  0.0 142.9 %stage.1 = bf16[128,4096]{1,0:T(8,128)(2,1)} custom-call(bf16[32,8,8,4096]{3,2,1,0:T(8,128)(2,1)} %bitcast.23, s32[8,128]{1,0:T(8,128)} %bitcast.29, s32[8,128]{1,0:T(8,128)} %bitcast.30, f32[8,128]{1,0:T(8,128)} %bitcast.31, bf16[128,4096]{1,0:T(8,128)(2,1)} %bitcast.28, f32[1,4096]{1,0:T(1,128)} %gain_moe.1, f32[1,4096]{1,0:T(1,128)} %gain_attn.1, ...), custom_call_target="tpu_custom_call" | custom-call | flops 40000000000 | bytes 180000000 | tf_op jit(solution)/shard_map/stage/pallas_call | solution.py:419
  142.9 2.3 %copy.16 = bf16[1,1,1,128,4096]{4,3,2,1,0:T(8,128)(2,1)} copy(bf16[1,1,1,128,4096]{4,3,2,1,0:T(8,128)(2,1)} %bitcast.27) | data formatting | bytes 2097152

commit v3 on v2

--- a/solution.py
+++ b/solution.py
@@ -19,8 +19,8 @@
 
 def stage_kernel(
     chunks, stages, chips,
-    eo, ids, slots, gates, resid_hbm, gain_moe, gain_attn, wg, wu, wd, wq, wk, wv, wo, out_hbm,
-    pool, nat, part, relay, final, r_ids, r_slots, r_gates, resid, normed, hidden, ysend, yin, kbuf,
+    eo, ids, slots, gates, resid_hbm, gain_moe_hbm, gain_attn_hbm, wg, wu, wd, wq, wk, wv, wo, out_hbm,
+    pool, nat, part, relay, final, r_ids, r_slots, r_gates, gain_moe, gain_attn, resid, normed, hidden, ysend, yin, kbuf,
     s_load, s_pool, s_nat, s_rows, s_rowx, s_route, r_route, s_msg, r_msg, s_y, r_y,
 ):
     toks, dim = resid.shape
@@ -51,19 +51,19 @@
     halves = (pl.ds(0, half), pl.ds(half, half))
     lo, hi = halves
 
+    barrier = pltpu.get_barrier_semaphore()
+    for peer in ({"ep": across}, {"ep": right}, {"ep": left}, {"ep": partner}, {"pp": nxt}, {"pp": prv}):
+        pl.semaphore_signal(barrier, inc=1, device_id=peer, device_id_type=MESH)
     own_loads = {}
     for k in order:
         own_loads[k] = [pltpu.make_async_copy(eo.at[:, at_chip(k, core), :, halves[h]],
                                               pool.at[2 * k + h, pl.ds(core * local_experts, local_experts)], s_load.at[2 * k + h])
                         for h in range(2)]
-    for copy in own_loads[2]:
+    small = [(resid_hbm, resid), (gain_moe_hbm, gain_moe), (gain_attn_hbm, gain_attn),
+             (ids, r_ids.at[0]), (slots, r_slots.at[0]), (gates, r_gates.at[0])]
+    small_loads = [pltpu.make_async_copy(src, dst, s_load.at[2 * chips + n]) for n, (src, dst) in enumerate(small)]
+    for copy in own_loads[2] + small_loads:
         copy.start()
-    resid_load = pltpu.make_async_copy(resid_hbm, resid, s_load.at[2 * chips])
-    resid_load.start()
-
-    barrier = pltpu.get_barrier_semaphore()
-    for peer in ({"ep": right}, {"ep": left}, {"ep": across}, {"ep": partner}, {"pp": nxt}, {"pp": prv}):
-        pl.semaphore_signal(barrier, inc=1, device_id=peer, device_id_type=MESH)
     pl.semaphore_wait(barrier, 6)
 
     routing = []
@@ -110,7 +110,8 @@
         inv = lax.rsqrt(jnp.mean(values * values, axis=-1, keepdims=True) + EPSILON)
         normed[at, :] = (values * inv * gain[...]).astype(BF16)
 
-    resid_load.wait()
+    for copy in small_loads:
+        copy.wait()
 
     def norm_resid(i, carry):
         norm_rows(resid, gain_moe, i)
@@ -120,12 +121,9 @@
 
     ncol = min(512, half)
 
-    def partial_sum(k):
+    def gate_matrix(k):
         dst = at_chip(k, core)
-        if k == 0:
-            e, s, g = ids[...], slots[...], gates[...]
-        else:
-            e, s, g = r_ids[k], r_slots[k], r_gates[k]
+        e, s, g = r_ids[k], r_slots[k], r_gates[k]
         where_row = jnp.where(s >= 0, (e - chip * (2 * local_experts)) * cap + s - dst * cap, -1)
         row_iota = lax.broadcasted_iota(jnp.int32, (depth, toks), 0)
         weight = jnp.zeros((depth, toks), F32)
@@ -136,17 +134,19 @@
         rest = weight - high.astype(F32)
         mid = rest.astype(BF16)
         low = (rest - mid.astype(F32)).astype(BF16)
-        for h in range(2):
-            def column(n, carry):
-                start = pl.multiple_of(n * ncol, ncol)
-                block = pool[2 * k + h, :, :, pl.ds(start, ncol)].reshape(depth, ncol)
-                total = jnp.dot(high, block, preferred_element_type=F32)
-                total += jnp.dot(mid, block, preferred_element_type=F32)
-                total += jnp.dot(low, block, preferred_element_type=F32)
-                part[k, :, pl.ds(pl.multiple_of(h * half + start, ncol), ncol)] = total
-                return carry
-
-            lax.fori_loop(0, half // ncol, column, 0)
+        return high, mid, low
+
+    def partial_sum(k, h, weights):
+        def column(n, carry):
+            start = pl.multiple_of(n * ncol, ncol)
+            block = pool[2 * k + h, :, :, pl.ds(start, ncol)].reshape(depth, ncol)
+            total = jnp.dot(weights[0], block, preferred_element_type=F32)
+            total += jnp.dot(weights[1], block, preferred_element_type=F32)
+            total += jnp.dot(weights[2], block, preferred_element_type=F32)
+            part[k, :, pl.ds(pl.multiple_of(h * half + start, ncol), ncol)] = total
+            return carry
+
+        lax.fori_loop(0, half // ncol, column, 0)
 
     def message(kind, t):
         tk = pl.ds(t * step_toks, step_toks)
@@ -164,56 +164,51 @@
         if t < chunks:
             message(kind, t).start()
 
-    def arrive(k, following):
+    def routing_arrived(k):
         for slot, copy in routing:
             if slot == k:
                 copy.wait_recv()
-        for copy in own_loads[k]:
-            copy.wait()
+
+    def rows_arrived(k, h):
+        own_loads[k][h].wait()
+        row_sends[k][h].wait_recv()
+
+    def start_rows(k):
         for copy in row_sends[k]:
-            copy.wait_recv()
-        if following is not None:
-            for copy in row_sends[following]:
-                copy.start()
+            copy.start()
 
     ahead = min(3, chunks)
-    arrive(2, 1)
+    routing_arrived(2)
+    weights = gate_matrix(2)
+    rows_arrived(2, 0)
+    start_rows(1)
+    partial_sum(2, 0, weights)
+    for t in range(ahead):
+        send(0, t)
+    rows_arrived(2, 1)
+    start_rows(3)
+    partial_sum(2, 1, weights)
+    for t in range(ahead):
+        send(1, t)
     for i in range(ksteps):
         for copy in load_gate_up(i):
             copy.start()
-    partial_sum(2)
-    for t in range(ahead):
-        send(0, t)
-        send(1, t)
-    arrive(1, 3)
-    partial_sum(1)
+    routing_arrived(1)
+    weights = gate_matrix(1)
+    rows_arrived(1, 0)
+    rows_arrived(1, 1)
+    start_rows(0)
+    for h in range(2):
+        partial_sum(1, h, weights)
     send(2, 0)
-    arrive(3, 0)
-    partial_sum(3)
+    routing_arrived(3)
+    weights = gate_matrix(3)
+    for h in range(2):
+        rows_arrived(3, h)
+        partial_sum(3, h, weights)
     send(3, 0)
     for n in range(2 * fsteps):
         load_rows(wd, n // fsteps, n % fsteps, 4 + n).start()
-
-    for i in range(ksteps):
-        for copy in load_gate_up(i):
-            copy.wait()
-        product = jnp.dot(normed[:, i * depth:(i + 1) * depth], pool[first_shared + i].reshape(depth, half), preferred_element_type=F32)
-        part[0, :, lo] = product if i == 0 else part[0, :, lo] + product
-    gate_act = part[0, :, pl.ds(0, ff)]
-    hidden[...] = (gate_act * jax.nn.sigmoid(gate_act) * part[0, :, pl.ds(ff, ff)]).astype(BF16)
-    arrive(0, None)
-    partial_sum(0)
-    for hh in range(2):
-        for i in range(fsteps):
-            load_rows(wd, hh, i, 4 + hh * fsteps + i).wait()
-        for n in range(half // ncol):
-            at = pl.ds(hh * half + n * ncol, ncol)
-            product = None
-            for i in range(fsteps):
-                block = pool[4 + hh * fsteps + i, :, :, pl.ds(n * ncol, ncol)].reshape(depth, ncol)
-                term = jnp.dot(hidden[:, i * depth:(i + 1) * depth], block, preferred_element_type=F32)
-                product = term if product is None else product + term
-            part[0, :, at] += resid[:, at].astype(F32) + product.astype(BF16).astype(F32)
 
     def forward(t):
         tk = pl.ds(t * step_toks, step_toks)
@@ -228,6 +223,33 @@
         send(0, t + ahead)
         send(1, t + ahead)
 
+    forward(0)
+
+    for i in range(ksteps):
+        for copy in load_gate_up(i):
+            copy.wait()
+        product = jnp.dot(normed[:, i * depth:(i + 1) * depth], pool[first_shared + i].reshape(depth, half), preferred_element_type=F32)
+        part[0, :, lo] = product if i == 0 else part[0, :, lo] + product
+    gate_act = part[0, :, pl.ds(0, ff)]
+    hidden[...] = (gate_act * jax.nn.sigmoid(gate_act) * part[0, :, pl.ds(ff, ff)]).astype(BF16)
+    weights = gate_matrix(0)
+    for h in range(2):
+        rows_arrived(0, h)
+        partial_sum(0, h, weights)
+    if chunks > 1:
+        forward(1)
+    for hh in range(2):
+        for i in range(fsteps):
+            load_rows(wd, hh, i, 4 + hh * fsteps + i).wait()
+        for n in range(half // ncol):
+            at = pl.ds(hh * half + n * ncol, ncol)
+            product = None
+            for i in range(fsteps):
+                block = pool[4 + hh * fsteps + i, :, :, pl.ds(n * ncol, ncol)].reshape(depth, ncol)
+                term = jnp.dot(hidden[:, i * depth:(i + 1) * depth], block, preferred_element_type=F32)
+                product = term if product is None else product + term
+            part[0, :, at] += resid[:, at].astype(F32) + product.astype(BF16).astype(F32)
+
     def shift(t):
         tk = pl.ds(t * step_toks, step_toks)
         return remote(ysend.at[tk], yin.at[tk], s_y.at[t], r_y.at[t], {"pp": nxt})
@@ -250,7 +272,7 @@
     def lay_out(j, carry):
         slot = lax.rem(j, nat_slots)
         load_heads(wq, j, slot).wait()
-        pool[j] = nat[slot].reshape(groups, cap, half)
+        pool.at[j][...] = nat.at[slot][...].reshape(groups, cap, half)
 
         @pl.when(j + nat_slots < slabs)
         def _():
@@ -264,7 +286,8 @@
     per_chunk = -(-slabs // max(1, chunks - 2))
     done = 0
     for t in range(chunks):
-        forward(t)
+        if t > 1:
+            forward(t)
         if t > 0:
             finish(t - 1)
         if t > 1:
@@ -308,7 +331,7 @@
                 j = hh * ksteps + i
                 slot = slot_of(j + (1 + which) * slabs)
                 load_heads(matrix, j, slot).wait()
-                part[2 + which, :, at] += jnp.dot(normed[:, pl.ds(pl.multiple_of(i * depth, depth), depth)], nat[slot].reshape(depth, half), preferred_element_type=F32)
+                part[2 + which, :, at] += jnp.dot(normed[:, pl.ds(pl.multiple_of(i * depth, depth), depth)], nat.at[slot][...].reshape(depth, half), preferred_element_type=F32)
                 nj = j + nat_slots
 
                 @pl.when(nj < slabs)
@@ -320,7 +343,7 @@
                     def _():
                         load_heads(following, nj - slabs, slot).start()
 
-                if which == 0 and hh == 0:
+                if which == 1 and hh == 1:
                     load_rows(wo, 1, i, ksteps + i).start()
                 return carry
 
@@ -392,7 +415,6 @@
     top_k = ids.shape[0]
     pool_slots = max(2 * dim // depth, 2 * chips + dim // depth)
     any_spec = pl.BlockSpec(memory_space=pl.ANY)
-    vmem = pl.BlockSpec(memory_space=pltpu.VMEM)
     dma = pltpu.SemaphoreType.DMA
     scratch = [
         pltpu.VMEM((pool_slots, groups, cap, half), BF16),
@@ -403,13 +425,15 @@
         pltpu.VMEM((chips, top_k, toks), jnp.int32),
         pltpu.VMEM((chips, top_k, toks), jnp.int32),
         pltpu.VMEM((chips, top_k, toks), F32),
+        pltpu.VMEM((1, dim), F32),
+        pltpu.VMEM((1, dim), F32),
         pltpu.VMEM((toks, dim), BF16),
         pltpu.VMEM((toks, dim), BF16),
         pltpu.VMEM((toks, ff), BF16),
         pltpu.VMEM((toks, dim), BF16),
         pltpu.VMEM((toks, dim), BF16),
         pltpu.VMEM((toks, dim), BF16),
-        dma((2 * chips + 1,)), dma((2, pool_slots)), dma((nat_slots,)), dma((2 * chips,)), dma((2 * chips,)),
+        dma((2 * chips + 6,)), dma((2, pool_slots)), dma((nat_slots,)), dma((2 * chips,)), dma((2 * chips,)),
         dma((chips, 3)), dma((chips, 3)), dma((6, chunks)), dma((6, chunks)), dma((chunks,)), dma((chunks,)),
     ]
 
@@ -419,7 +443,7 @@
     return pl.pallas_call(
         functools.partial(stage_kernel, chunks, stages, chips),
         out_shape=jax.ShapeDtypeStruct((toks, dim), BF16),
-        in_specs=[any_spec, vmem, vmem, vmem, any_spec, vmem, vmem] + [any_spec] * 7,
+        in_specs=[any_spec] * 14,
         out_specs=any_spec,
         scratch_shapes=scratch,
         cost_estimate=pl.CostEstimate(flops=40_000_000_000, bytes_accessed=180_000_000, transcendentals=0),

time: 145 us -> 137 us (0.945)
  Pallas kernels: 143 us -> 135 us
    pallas_call x1, Pallas kernels: 143 us -> 135 us  [run_stage(): pl.pallas_call(functools.partial(stage_kernel, chunks, stages, chips), ou...]
where the time goes in v3:
time: 137 us
  Pallas kernels  135 us (99%)
  local copies, waits for them, and re-layouts  2.29 us (2%)
    pallas_call x1, Pallas kernels, run_stage(): pl.pallas_call(functools.partial(stage_kernel, chunks, stages, chips), ou...  135 us

profile of v3, /device:TPU:97, one launch (start us, length us, event | category | flops | bytes accessed | tf_op | source)
XLA Modules:
  0.0 137.2 jit_solution(149572884835427756)
XLA Ops:
  0.0 134.9 %stage.1 = bf16[128,4096]{1,0:T(8,128)(2,1)} custom-call(bf16[32,8,8,4096]{3,2,1,0:T(8,128)(2,1)} %bitcast.23, s32[8,128]{1,0:T(8,128)} %bitcast.29, s32[8,128]{1,0:T(8,128)} %bitcast.30, f32[8,128]{1,0:T(8,128)} %bitcast.31, bf16[128,4096]{1,0:T(8,128)(2,1)} %bitcast.28, f32[1,4096]{1,0:T(1,128)} %gain_moe_hbm.1, f32[1,4096]{1,0:T(1,128)} %gain_attn_hbm.1, ...), custom_call_target="tpu_custom_call" | custom-call | flops 40000000000 | bytes 180000000 | tf_op jit(solution)/shard_map/stage/pallas_call | solution.py:443
  134.9 2.3 %copy.16 = bf16[1,1,1,128,4096]{4,3,2,1,0:T(8,128)(2,1)} copy(bf16[1,1,1,128,4096]{4,3,2,1,0:T(8,128)(2,1)} %bitcast.27) | data formatting | bytes 2097152

commit v4 on v3

--- a/solution.py
+++ b/solution.py
@@ -17,12 +17,14 @@
     return pltpu.make_async_remote_copy(src_ref=src, dst_ref=dst, send_sem=send, recv_sem=recv, device_id=where, device_id_type=MESH)
 
 
-def stage_kernel(
-    chunks, stages, chips,
-    eo, ids, slots, gates, resid_hbm, gain_moe_hbm, gain_attn_hbm, wg, wu, wd, wq, wk, wv, wo, out_hbm,
-    pool, nat, part, relay, final, r_ids, r_slots, r_gates, gain_moe, gain_attn, resid, normed, hidden, ysend, yin, kbuf,
-    s_load, s_pool, s_nat, s_rows, s_rowx, s_route, r_route, s_msg, r_msg, s_y, r_y,
-):
+def stage_kernel(nat_shape, chunks, stages, chips, *refs):
+    pl.run_scoped(functools.partial(stage_body, chunks, stages, chips, refs), pltpu.VMEM(nat_shape, BF16))
+
+
+def stage_body(chunks, stages, chips, refs, nat):
+    (eo, ids, slots, gates, resid_hbm, gain_moe_hbm, gain_attn_hbm, wg, wu, wd, wq, wk, wv, wo, out_hbm, key_hbm,
+        pool, part, relay, final, r_ids, r_slots, r_gates, gain_moe, gain_attn, resid, normed, hidden, ysend, yin, kbuf,
+        s_load, s_pool, s_nat, s_back, s_rows, s_rowx, s_route, r_route, s_msg, r_msg, s_y, r_y) = refs
     toks, dim = resid.shape
     half = dim // 2
     groups = pool.shape[1]
@@ -177,7 +179,7 @@
         for copy in row_sends[k]:
             copy.start()
 
-    ahead = min(3, chunks)
+    ahead = min(5, chunks)
     routing_arrived(2)
     weights = gate_matrix(2)
     rows_arrived(2, 0)
@@ -266,24 +268,42 @@
         for i in range(step_toks // blk):
             norm_rows(yin, gain_attn, t * (step_toks // blk) + i)
 
+    sources = (wk, wq, wv)
+
+    def back(j):
+        return pltpu.make_async_copy(pool.at[j], key_hbm.at[j], s_back.at[j])
+
     for slot in range(nat_slots):
-        load_heads(wq, slot, slot).start()
-
-    def lay_out(j, carry):
-        slot = lax.rem(j, nat_slots)
-        load_heads(wq, j, slot).wait()
-        pool.at[j][...] = nat.at[slot][...].reshape(groups, cap, half)
-
-        @pl.when(j + nat_slots < slabs)
+        load_heads(wk, slot, slot).start()
+
+    def next_load(which, j, slot):
+        nj = j + nat_slots
+
+        @pl.when(nj < slabs)
         def _():
-            load_heads(wq, j + nat_slots, slot).start()
-
-        @pl.when(j + nat_slots >= slabs)
-        def _():
-            load_heads(wk, j + nat_slots - slabs, slot).start()
-        return carry
-
-    per_chunk = -(-slabs // max(1, chunks - 2))
+            load_heads(sources[which], nj, slot).start()
+
+        if which + 1 < len(sources):
+            @pl.when(nj >= slabs)
+            def _():
+                load_heads(sources[which + 1], nj - slabs, slot).start()
+
+    def lay_out(which, begin, end):
+        def step(j, carry):
+            slot = lax.rem(j + which * slabs, nat_slots)
+            load_heads(sources[which], j, slot).wait()
+            if which == 1:
+                back(j).wait()
+            pool.at[j][...] = nat.at[slot][...].reshape(groups, cap, half)
+            if which == 0:
+                back(j).start()
+            next_load(which, j, slot)
+            return carry
+
+        if end > begin:
+            lax.fori_loop(begin, end, step, 0)
+
+    per_chunk = -(-2 * slabs // max(1, chunks - 3))
     done = 0
     for t in range(chunks):
         if t > 1:
@@ -292,10 +312,11 @@
             finish(t - 1)
         if t > 1:
             receive(t - 2)
-        upto = min(slabs, done + per_chunk) if t < chunks - 1 else slabs
-        if upto > done:
-            lax.fori_loop(done, upto, lay_out, 0)
-        done = upto
+        if t > 1 or chunks < 4:
+            upto = min(2 * slabs, done + per_chunk) if t < chunks - 1 else 2 * slabs
+            lay_out(0, done, min(upto, slabs))
+            lay_out(1, max(done, slabs) - slabs, upto - slabs)
+            done = upto
     if chunks > 1:
         receive(chunks - 2)
     finish(chunks - 1)
@@ -309,52 +330,49 @@
 
     qbuf, vbuf = resid, ysend
 
+    def load_key(s_idx):
+        return pltpu.make_async_copy(key_hbm.at[s_idx], pool.at[s_idx], s_pool.at[0, s_idx])
+
+    def inputs(i):
+        return normed[:, pl.ds(pl.multiple_of(i * depth, depth), depth)]
+
     def query(i, carry):
         for hh in range(2):
-            at = halves[hh]
-            product = jnp.dot(normed[:, pl.ds(pl.multiple_of(i * depth, depth), depth)], pool[hh * ksteps + i].reshape(depth, half), preferred_element_type=F32)
-            part[1, :, at] += product
-        load_rows(wo, 0, i, i).start()
+            part[1, :, halves[hh]] += jnp.dot(inputs(i), pool[hh * ksteps + i].reshape(depth, half), preferred_element_type=F32)
+        load_key(i).start()
         return carry
 
     lax.fori_loop(0, ksteps, query, 0)
     qbuf[...] = part[1].astype(BF16)
 
-    def slot_of(index):
-        return lax.rem(index, nat_slots)
-
-    def stream(which, matrix, following):
-        for hh in range(2):
-            at = halves[hh]
-
-            def step(i, carry):
-                j = hh * ksteps + i
-                slot = slot_of(j + (1 + which) * slabs)
-                load_heads(matrix, j, slot).wait()
-                part[2 + which, :, at] += jnp.dot(normed[:, pl.ds(pl.multiple_of(i * depth, depth), depth)], nat.at[slot][...].reshape(depth, half), preferred_element_type=F32)
-                nj = j + nat_slots
-
-                @pl.when(nj < slabs)
-                def _():
-                    load_heads(matrix, nj, slot).start()
-
-                if following is not None:
-                    @pl.when(nj >= slabs)
-                    def _():
-                        load_heads(following, nj - slabs, slot).start()
-
-                if which == 1 and hh == 1:
-                    load_rows(wo, 1, i, ksteps + i).start()
-                return carry
-
-            lax.fori_loop(0, ksteps, step, 0)
-
-    stream(0, wk, wv)
-    kbuf[...] = part[2].astype(BF16)
-    stream(1, wv, None)
+    for hh in range(2):
+        def value(i, carry):
+            j = hh * ksteps + i
+            slot = lax.rem(j + 2 * slabs, nat_slots)
+            load_heads(wv, j, slot).wait()
+            part[3, :, halves[hh]] += jnp.dot(inputs(i), nat.at[slot][...].reshape(depth, half), preferred_element_type=F32)
+            next_load(2, j, slot)
+
+            @pl.when(lax.rem(j, 2) == 1)
+            def _():
+                load_key(ksteps + lax.div(j, 2)).start()
+            return carry
+
+        lax.fori_loop(0, ksteps, value, 0)
     for t in range(chunks):
         shift(t).wait_send()
     vbuf[...] = part[3].astype(BF16)
+
+    for hh in range(2):
+        def key(i, carry):
+            j = hh * ksteps + i
+            load_key(j).wait()
+            part[2, :, halves[hh]] += jnp.dot(inputs(i), pool[j].reshape(depth, half), preferred_element_type=F32)
+            load_rows(wo, hh, i, j).start()
+            return carry
+
+        lax.fori_loop(0, ksteps, key, 0)
+    kbuf[...] = part[2].astype(BF16)
 
     scale = 1.0 / math.sqrt(head_dim)
     causal = lax.broadcasted_iota(jnp.int32, (toks, toks), 0) >= lax.broadcasted_iota(jnp.int32, (toks, toks), 1)
@@ -418,7 +436,6 @@
     dma = pltpu.SemaphoreType.DMA
     scratch = [
         pltpu.VMEM((pool_slots, groups, cap, half), BF16),
-        pltpu.VMEM((nat_slots, depth, heads // 2, head_dim), BF16),
         pltpu.VMEM((chips, toks, dim), F32),
         pltpu.VMEM((2, toks, half), F32),
         pltpu.VMEM((2, toks, dim), F32),
@@ -433,7 +450,7 @@
         pltpu.VMEM((toks, dim), BF16),
         pltpu.VMEM((toks, dim), BF16),
         pltpu.VMEM((toks, dim), BF16),
-        dma((2 * chips + 6,)), dma((2, pool_slots)), dma((nat_slots,)), dma((2 * chips,)), dma((2 * chips,)),
+        dma((2 * chips + 6,)), dma((2, pool_slots)), dma((nat_slots,)), dma((pool_slots,)), dma((2 * chips,)), dma((2 * chips,)),
         dma((chips, 3)), dma((chips, 3)), dma((6, chunks)), dma((6, chunks)), dma((chunks,)), dma((chunks,)),
     ]
 
@@ -441,15 +458,15 @@
         return matrix.reshape(-1, cap, matrix.shape[-1])
 
     return pl.pallas_call(
-        functools.partial(stage_kernel, chunks, stages, chips),
-        out_shape=jax.ShapeDtypeStruct((toks, dim), BF16),
+        functools.partial(stage_kernel, (nat_slots, depth, heads // 2, head_dim), chunks, stages, chips),
+        out_shape=(jax.ShapeDtypeStruct((toks, dim), BF16), jax.ShapeDtypeStruct((2 * dim // depth, groups, cap, half), BF16)),
         in_specs=[any_spec] * 14,
-        out_specs=any_spec,
+        out_specs=(any_spec, any_spec),
         scratch_shapes=scratch,
         cost_estimate=pl.CostEstimate(flops=40_000_000_000, bytes_accessed=180_000_000, transcendentals=0),
         compiler_params=pltpu.CompilerParams(collective_id=0, has_side_effects=True, vmem_limit_bytes=67_043_328),
         name="stage",
-    )(eo, ids, slots, gates, resid, gain_moe, gain_attn, grouped(wg), grouped(wu), grouped(wd), wq, wk, wv, grouped(wo))
+    )(eo, ids, slots, gates, resid, gain_moe, gain_attn, grouped(wg), grouped(wu), grouped(wd), wq, wk, wv, grouped(wo))[0]
 
 
 def solution(mesh):

time: 137 us -> 129 us (0.942)
  the two profiles are of different devices: /device:TPU:97 before, /device:TPU:96 now
where the time goes in v4:
time: 129 us
  Pallas kernels  127 us (98%)
  local copies, waits for them, and re-layouts  2.29 us (2%)
    pallas_call x1, Pallas kernels, run_stage(): pl.pallas_call(functools.partial(stage_kernel, (nat_slots, depth, heads /...  127 us

profile of v4, /device:TPU:96, one launch (start us, length us, event | category | flops | bytes accessed | tf_op | source)
XLA Modules:
  0.0 129.2 jit_solution(4265155707466140706)
XLA Ops:
  0.0 126.9 %stage.1 = (bf16[128,4096]{1,0:T(8,128)(2,1)}, bf16[16,64,8,2048]{3,2,1,0:T(8,128)(2,1)}) custom-call(bf16[32,8,8,4096]{3,2,1,0:T(8,128)(2,1)} %bitcast.23, s32[8,128]{1,0:T(8,128)} %bitcast.29, s32[8,128]{1,0:T(8,128)} %bitcast.30, f32[8,128]{1,0:T(8,128)} %bitcast.31, bf16[128,4096]{1,0:T(8,128)(2,1)} %bitcast.27, f32[1,4096]{1,0:T(1,128)} %refs_5_.1, ...), custom_call_target="tpu_custom_call" | custom-call | flops 40000000000 | bytes 180000000 | tf_op jit(solution)/shard_map/stage/pallas_call | solution.py:460
  126.9 2.3 %copy.16 = bf16[1,1,1,128,4096]{4,3,2,1,0:T(8,128)(2,1)} copy(bf16[1,1,1,128,4096]{4,3,2,1,0:T(8,128)(2,1)} %bitcast.28) | data formatting | bytes 2097152
